TPU v7x, 256 devices: a whole 4x4x8 slice. The times are simulated.
256 devices in a mesh: seq: 64 (over y, z, core), tp: 4 (over x).
Axes of the slice: x: 4, y: 4, z: 8, core: 2. Of those that a mesh axis runs over, the one named last changes fastest.
Arguments:
- tokens: bfloat16 [49152, 4096], P('seq'), may hold values from -6 to 6
- query_weight: bfloat16 [4096, 2048], P('seq', 'tp'), may hold values from -0.09375 to 0.09375
- key_weight: bfloat16 [4096, 2048], P('seq', 'tp'), may hold values from -0.09375 to 0.09375
- value_weight: bfloat16 [4096, 2048], P('seq', 'tp'), may hold values from -0.09375 to 0.09375
- gate_weight: bfloat16 [4096, 16], P('seq', 'tp'), may hold values from -0.09375 to 0.09375
- decay_rate: float32 [16], P('tp'), may hold values from 4.0690106e-06 to 0.04
- norm_gain: float32 [2048], P('tp'), may hold values from 0.5 to 1.5
- out_weight: bfloat16 [2048, 4096], P(None, 'tp'), may hold values from -0.125 to 0.125
Outputs:
- mixed: bfloat16 [49152, 4096], P('seq', 'tp')
All inputs are finite; a program needn't handle non-finite values.
Results may differ from a plain program's by a relative error of at most 0.006.
The roundings to bfloat16 on the way count: a program that leaves them out, or rounds other values in their place, can miss the bound.
Values may be sent and summed in bfloat16 or wider, within the bound.
A program may use at most 128 MiB of HBM per device.

v0:
```python
import jax
import jax.numpy as jnp
from jax import lax
from jax.sharding import Mesh
from jax.sharding import PartitionSpec as P

SEQ = ("seq_0", "seq_1", "seq_2")


def side_by_side(arrays, axis, dim, along):
    both = jnp.concatenate(arrays, axis=along)
    whole, at, finished = (lax.all_gather(both, axis, axis=dim, tiled=True), 0, [])
    for a in arrays:
        finished.append(lax.slice_in_dim(whole, at, at + a.shape[along], axis=along))
        at += a.shape[along]
    return tuple(finished)


def nothing_yet(shard, identity):
    return jax.tree.map(
        lambda part, zero: jnp.zeros_like(part) + jnp.asarray(zero, part.dtype), shard, identity
    )


def carried_in(shard, axes, combine, identity):
    before = start = nothing_yet(shard, identity)
    so_far = shard
    for axis in reversed(axes):
        peers, position = (lax.axis_size(axis), lax.axis_index(axis))
        pieces = jax.tree.map(lambda part: lax.all_gather(part, axis), so_far)
        inside, so_far = (start, start)
        for k in range(peers):
            passed = k < position
            so_far = combine(so_far, jax.tree.map(lambda part: part[k], pieces))
            inside = jax.tree.map(lambda new, old: jnp.where(passed, new, old), so_far, inside)
        before = combine(inside, before)
    return before


def on_device(
    tokens, query_weight, key_weight, value_weight, gate_weight, decay_rate, norm_gain, out_weight
):
    tok_rows = tokens.shape[0]
    head_count = decay_rate.shape[0]
    proj_width = query_weight.shape[1]
    head_size = proj_width // head_count

    def contract(piece):
        return jnp.dot(tokens, piece, preferred_element_type=jnp.float32)

    pieces = side_by_side((query_weight, key_weight, value_weight, gate_weight), SEQ, 0, 1)
    query_proj, key_proj, value_proj, gate_logit = tuple(
        (contract(one_piece) for one_piece in pieces)
    )
    query_heads = query_proj.astype(jnp.bfloat16).reshape(tok_rows, head_count, head_size)
    key_heads = key_proj.astype(jnp.bfloat16).reshape(tok_rows, head_count, head_size)
    value_per_head = value_proj.astype(jnp.bfloat16).reshape(tok_rows, head_count, head_size)
    log_decay = -decay_rate[None, :] * jax.nn.softplus(gate_logit)
    within = jnp.cumsum(log_decay, axis=0)
    block_total = within[-1]
    key_scaled = (jnp.exp(block_total[None, :] - within)[:, :, None] * key_heads).astype(
        jnp.bfloat16
    )
    shard_local_state = jnp.einsum(
        "gfw,gfz->fwz", key_scaled, value_per_head, preferred_element_type=jnp.float32
    )

    def decayed_join(earlier, later):
        return (earlier[0] + later[0], jnp.exp(later[0])[:, None, None] * earlier[1] + later[1])

    _, prefix_state = carried_in(
        (block_total, shard_local_state),
        SEQ,
        decayed_join,
        (jnp.zeros_like(block_total), jnp.zeros_like(shard_local_state)),
    )
    query_scaled = (jnp.exp(within)[:, :, None] * query_heads).astype(jnp.bfloat16)
    carried_state = jnp.einsum(
        "fys,ysu->fyu",
        query_scaled,
        prefix_state.astype(jnp.bfloat16),
        preferred_element_type=jnp.float32,
    )
    scores = jnp.einsum("thk,shk->hts", query_heads, key_heads, preferred_element_type=jnp.float32)
    row_index = lax.broadcasted_iota(jnp.int32, (tok_rows, tok_rows), 0)
    col_index = lax.broadcasted_iota(jnp.int32, (tok_rows, tok_rows), 1)
    causal = (col_index <= row_index)[None, :, :]
    decay_gap = within.T[:, :, None] - within.T[:, None, :]
    attn = jnp.where(causal, scores * jnp.exp(jnp.where(causal, decay_gap, 0.0)), 0.0).astype(
        jnp.bfloat16
    )
    local_part = jnp.einsum(
        "hts,shv->thv", attn, value_per_head, preferred_element_type=jnp.float32
    )
    head_out = carried_state + local_part
    mean_square = jnp.mean(head_out * head_out, axis=-1, keepdims=True)
    normed = (head_out * lax.rsqrt(mean_square + 1e-05)).reshape(tok_rows, proj_width) * norm_gain[
        None, :
    ]
    normed = normed.astype(jnp.bfloat16)
    mixed = jnp.dot(
        lax.all_gather(normed, "tp", axis=1, tiled=True),
        out_weight,
        preferred_element_type=jnp.float32,
    )
    return mixed.astype(jnp.bfloat16)


def solution(mesh):
    finer = Mesh(mesh.devices.reshape(4, 8, 2, mesh.shape["tp"]), ("seq_0", "seq_1", "seq_2", "tp"))
    return jax.shard_map(
        on_device,
        mesh=finer,
        in_specs=(
            P(SEQ, None),
            P(SEQ, "tp"),
            P(SEQ, "tp"),
            P(SEQ, "tp"),
            P(SEQ, "tp"),
            P("tp"),
            P("tp"),
            P(None, "tp"),
        ),
        out_specs=P(SEQ, "tp"),
        check_vma=False,
    )
```

profile of v0, /device:TPU:1, one launch (start us, length us, event | category | flops | bytes accessed | tf_op | source)
XLA Modules:
  0.0 258.8 jit_solution(4576178796495780604)
XLA Ops:
  6.5 0.8 copy.26
  7.3 1.6 pad_maximum_fusion
  9.0 0.7 neg.9
  9.7 96.5 %all-gather.9.cloned.1.call-done = bf16[4096,1540]{1,0:T(8,128)(2,1)} async-done(((bf16[64,1540]{1,0:T(8,128)(2,1)}), bf16[4096,1540]{1,0:T(8,128)(2,1)}) %all-gather.9.cloned.1.call-update) | async-done | bytes 12615696 | tf_op jit(solution)/shard_map/all_gather | solution.py:12
  106.2 5.0 %fusion.70 = f32[4,768]{1,0:T(4,128)S(1)} fusion(bf16[768,4096]{1,0:T(8,128)(2,1)} %param.8, bf16[4096,1540]{1,0:T(8,128)(2,1)} %all-gather.9.cloned.1.call-done, f32[4]{0:T(128)S(1)} %neg.9), kind=kOutput, calls=%fused_computation.90 | convolution fusion | flops 25187328 | bytes 7352336 | tf_op jit(solution)/shard_map/dot_general | solution.py:49
  111.2 1.1 reduce-window.6
  112.4 0.2 slice_reduce_fusion
  112.5 0.2 reduce-window.9
  112.7 0.1 add_bitcast_fusion
  112.8 0.2 slice_reduce_fusion.1
  113.0 0.1 subtract_exponential_fusion
  113.1 7.7 %fusion.15 = bf16[512,768]{1,0:T(8,128)(2,1)S(1)} fusion(bf16[768,4096]{1,0:T(8,128)(2,1)} %param.8, bf16[4096,1540]{1,0:T(8,128)(2,1)} %all-gather.9.cloned.1.call-done), kind=kOutput, calls=%fused_computation.21 | convolution fusion | flops 3221618688 | bytes 11272192 | tf_op jit(solution)/shard_map/dot_general | solution.py:49
  120.8 5.9 %fusion.12 = bf16[512,768]{1,0:T(8,128)(2,1)S(1)} fusion(bf16[768,4096]{1,0:T(8,128)(2,1)S(1)} %bitcast.238, bf16[4096,1540]{1,0:T(8,128)(2,1)} %all-gather.9.cloned.1.call-done), kind=kOutput, calls=%fused_computation.20 | convolution fusion | flops 3221618688 | bytes 11272192 | tf_op jit(solution)/shard_map/dot_general | solution.py:49
  126.8 0.4 fusion.23
  127.1 2.2 all-gather
  129.3 1.8 all-gather.1
  131.1 0.8 bitcast_add_fusion.8
  132.0 0.2 iota_compare_fusion
  132.2 11.1 %all-gather.2 = f32[8,1,4]{2,1,0:T(1,128)S(1)} all-gather(f32[1,1,4]{2,1,0:T(1,128)S(1)} %get-tuple-element.23), channel_id=1, replica_groups=mesh['seq_0'=4,'seq_1'=8,'seq_2'=2,'tp'=4] {'seq_1'}, dimensions={0}, use_global_device_ids=true | all-gather | bytes 144 | tf_op jit(solution)/shard_map/all_gather | solution.py:30
  143.4 22.0 %all-gather.11.cloned.1.call-done = f32[8,4,128,128]{3,2,1,0:T(8,128)} async-done(((f32[1,4,128,128]{3,2,1,0:T(8,128)}), f32[8,4,128,128]{3,2,1,0:T(8,128)}) %all-gather.11.cloned.1.call-update) | async-done | bytes 2097168 | tf_op jit(solution)/shard_map/all_gather | solution.py:30
  165.4 2.4 multiply_add_fusion
  167.8 0.2 all-gather.15.cloned.1.call-start
  168.0 7.5 %fusion.18 = bf16[512,768]{1,0:T(8,128)(2,1)S(1)} fusion(bf16[768,4096]{1,0:T(8,128)(2,1)} %param.8, bf16[4096,1540]{1,0:T(8,128)(2,1)} %all-gather.9.cloned.1.call-done), kind=kOutput, calls=%fused_computation.22 | convolution fusion | flops 3221618688 | bytes 11272192 | tf_op jit(solution)/shard_map/dot_general | solution.py:49
  175.6 7.7 %all-gather.3 = f32[4,1,4]{2,1,0:T(1,128)S(1)} all-gather(f32[1,1,4]{2,1,0:T(1,128)S(1)} %get-tuple-element.10), channel_id=1, replica_groups=mesh['seq_0'=4,'seq_1'=8,'seq_2'=2,'tp'=4] {'seq_0'}, dimensions={0}, use_global_device_ids=true | all-gather | bytes 80 | tf_op jit(solution)/shard_map/all_gather | solution.py:30
  183.2 0.4 copy.28
  183.7 6.7 %fusion = f32[4,128,768]{2,1,0:T(8,128)} fusion(bf16[768,4,128]{0,2,1:T(8,128)(2,1)} %bitcast.245, f32[4,768]{1,0:T(4,128)S(1)} %get-tuple-element.9, pred[768,768]{1,0:T(8,128)(4,1)S(1)} %iota_compare_fusion, bf16[768,4,128]{0,2,1:T(8,128)(2,1)S(1)} %bitcast.240, bf16[768,4,128]{0,2,1:T(8,128)(2,1)} %bitcast.247), kind=kOutput, calls=%fused_computation.1 | convolution fusion | flops 1219756032 | bytes 4534272 | tf_op jit(solution)/shard_map/hts,shv->thv/dot_general | solution.py:92
  190.3 5.0 %all-gather.13.cloned.1.call-done = f32[4,4,128,128]{3,2,1,0:T(8,128)} async-done(((f32[1,4,128,128]{3,2,1,0:T(8,128)}), f32[4,4,128,128]{3,2,1,0:T(8,128)}) %all-gather.13.cloned.1.call-update) | async-done | bytes 1048592 | tf_op jit(solution)/shard_map/all_gather | solution.py:30
  195.3 3.5 %fusion.11 = (f32[768,4]{0,1:T(4,128)S(1)}, f32[4,128,768]{2,1,0:T(8,128)S(1)}) fusion(f32[4,128,768]{2,1,0:T(8,128)} %fusion, bf16[768,4,128]{2,0,1:T(8,128)(2,1)S(1)} %copy.28, f32[768,4]{0,1:T(4,128)S(1)} %get-tuple-element.8, f32[4,4,128,128]{3,2,1,0:T(8,128)} %all-gather.13.cloned.1.call-done, f32[8,4,128,128]{3,2,1,0:T(8,128)} %all-gather.11.cloned.1.call-done, ...), kind=kOutput, calls=%fused_computation.16 | convolution fusion | flops 105903104 | bytes 7627022 | tf_op jit(solution)/shard_map/fys,ysu->fyu/dot_general | solution.py:78
  198.9 0.1 bitcast_multiply_fusion.1
  199.0 1.0 fusion.10
  200.1 44.4 %all-gather.15.cloned.1.call-done = bf16[768,2048]{0,1:T(8,128)(2,1)} async-done(((bf16[768,512]{0,1:T(8,128)(2,1)}), bf16[768,2048]{0,1:T(8,128)(2,1)}) %all-gather.15.cloned.1.call-update) | async-done | bytes 3145744 | tf_op jit(solution)/shard_map/all_gather | solution.py:102
  244.5 7.8 %convolution_convert_fusion = bf16[768,1024]{1,0:T(8,128)(2,1)} fusion(bf16[768,2048]{0,1:T(8,128)(2,1)} %all-gather.15.cloned.1.call-done, bf16[2048,1024]{1,0:T(8,128)(2,1)} %param.15), kind=kOutput, calls=%fused_computation.11 | convolution fusion | flops 3222011904 | bytes 8912896 | tf_op jit(solution)/shard_map/dot_general | solution.py:101
  (27 shorter events, 0.3 us)
Async XLA Ops:
  6.5 99.7 %all-gather.9.cloned.1.call-start = ((), (), s32[]{:S(2)}) async-start(), calls=%async_computation | async-start | bytes 13844480 | tf_op jit(solution)/shard_map/all_gather | solution.py:12
  8.9 156.4 %all-gather.11.cloned.1.call-start = ((), (), s32[]{:S(2)}) async-start(), calls=%async_computation.1 | async-start | bytes 2359296 | tf_op jit(solution)/shard_map/all_gather | solution.py:30
  106.2 14.6 %slice-start = ((s8[6291456]{0:T(1024)(128)(4,1)}), s8[2097152]{0:T(1024)(128)(4,1)S(1)}, s32[]{:S(2)}) async-start(s8[6291456]{0:T(1024)(128)(4,1)} %bitcast.237), calls=%async_computation.4 | async-start | bytes 4194304
  113.1 7.7 %slice-start.1 = ((s8[6291456]{0:T(1024)(128)(4,1)}), s8[4194304]{0:T(1024)(128)(4,1)S(1)}, s32[]{:S(2)}) async-start(s8[6291456]{0:T(1024)(128)(4,1)} %bitcast.237), calls=%async_computation.5 | async-start | bytes 8388608
  120.8 6.0 %copy-start.1 = (bf16[512,768]{1,0:T(8,128)(2,1)}, bf16[512,768]{1,0:T(8,128)(2,1)S(1)}, u32[]{:S(2)}) copy-start(bf16[512,768]{1,0:T(8,128)(2,1)S(1)} %fusion.15) | copy-start | bytes 2359300
  126.7 4.4 %copy-start.2 = (bf16[512,768]{1,0:T(8,128)(2,1)}, bf16[512,768]{1,0:T(8,128)(2,1)S(1)}, u32[]{:S(2)}) copy-start(bf16[512,768]{1,0:T(8,128)(2,1)S(1)} %fusion.12) | copy-start | bytes 2359300
  131.9 63.4 %all-gather.13.cloned.1.call-start = ((), (), s32[]{:S(2)}) async-start(), calls=%async_computation.2 | async-start | bytes 1310720 | tf_op jit(solution)/shard_map/all_gather | solution.py:30
  167.8 76.7 %all-gather.15.cloned.1.call-start = ((), (), s32[]{:S(2)}) async-start(), calls=%async_computation.3 | async-start | bytes 3932160 | tf_op jit(solution)/shard_map/all_gather | solution.py:102
  195.3 3.7 %copy-start = (f32[512]{0:T(512)S(1)}, f32[512]{0:T(512)}, u32[]{:S(2)}) copy-start(f32[512]{0:T(512)} %param.14) | copy-start | bytes 6148
Sparse Core Ops, SparseCore 0:
  10.1 96.0 all-gather.8
  132.1 33.2 all-gather.10
  167.9 27.3 all-gather.12
  200.2 44.2 all-gather.14
where the time goes:
time: 259 us
  waiting for transfers between devices  168 us (65%)
  matrix products  44.5 us (17%)
  blocking collectives  22.8 us (9%)
  between operations  13.3 us (5%)
  other arithmetic  8.38 us (3%)
    all_gather x1, waiting for transfers between devices, side_by_side(): lax.all_gather(both, axis, axis=dim, tiled=True)  96.5 us
    all_gather x1, waiting for transfers between devices, on_device(): lax.all_gather(normed, 'tp', axis=1, tiled=True)  44.4 us
    all_gather x2, waiting for transfers between devices, carried_in(): pieces = jax.tree.map(lambda part: lax.all_gather(part, axis), so_far)  27 us
    dot_general x4, matrix products, contract(): return jnp.dot(tokens, piece, preferred_element_type=jnp.float32)  26.1 us
    all_gather x4, blocking collectives, carried_in(): pieces = jax.tree.map(lambda part: lax.all_gather(part, axis), so_far)  22.8 us
    dot_general x1, matrix products, on_device(): jnp.dot(lax.all_gather(normed, 'tp', axis=1, tiled=True), out_weight, pre...  7.75 us
    dot_general x1, matrix products, on_device(): jnp.einsum('hts,shv->thv', attn, value_per_head, preferred_element_type=j...  6.66 us
  transfers between devices with their start and end apart: 4, of which 4 were waited for; matrix products, arithmetic and copies ran while one was open for 6% of the time, Pallas kernels for 0%

commit v1 on v0

--- a/solution.py
+++ b/solution.py
@@ -5,6 +5,34 @@
 from jax.sharding import PartitionSpec as P
 
 SEQ = ("seq_0", "seq_1", "seq_2")
+
+
+def trace_spot(unit):
+    net_axis = "tp"
+    field_out, local_next, wide_out = (
+        lax.axis_size(net_axis),
+        lax.axis_index(net_axis),
+        unit.shape[1],
+    )
+    lanes = [(m, (m + 1) % field_out) for m in range(field_out)]
+    gallery = [(m, (m - 1) % field_out) for m in range(field_out)]
+    high = jnp.zeros((*unit.shape[:1], field_out * wide_out, *unit.shape[2:]), unit.dtype)
+    high = lax.dynamic_update_slice_in_dim(high, unit, local_next * wide_out, axis=1)
+    n_now = field_out // 2
+    it = 1
+    part_now = kept_arr = unit
+    while it < n_now + 1:
+        part_now = lax.ppermute(part_now, axis_name=net_axis, perm=lanes)
+        high = lax.dynamic_update_slice_in_dim(
+            high, part_now, (local_next - it) % field_out * wide_out, axis=1
+        )
+        if it < field_out - n_now:
+            kept_arr = lax.ppermute(kept_arr, net_axis, gallery)
+            high = lax.dynamic_update_slice_in_dim(
+                high, kept_arr, (local_next + it) % field_out * wide_out, axis=1
+            )
+        it += 1
+    return high
 
 
 def side_by_side(arrays, axis, dim, along):
@@ -98,11 +126,7 @@
         None, :
     ]
     normed = normed.astype(jnp.bfloat16)
-    mixed = jnp.dot(
-        lax.all_gather(normed, "tp", axis=1, tiled=True),
-        out_weight,
-        preferred_element_type=jnp.float32,
-    )
+    mixed = jnp.dot(trace_spot(normed), out_weight, preferred_element_type=jnp.float32)
     return mixed.astype(jnp.bfloat16)
 
 

time: 259 us -> 251 us (0.969); the launches traced: 259 us -> 248 us
  waiting for transfers between devices: 168 us -> 153 us
  local copies, waits for them, and re-layouts: 1.55 us -> 5.96 us
  matrix products: 44.5 us -> 41.2 us
    all_gather x1 -> x0, waiting for transfers between devices: 44.4 us -> none  [on_device(): lax.all_gather(normed, 'tp', axis=1, tiled=True)]
    ppermute x0 -> x3, waiting for transfers between devices: none -> 29.5 us  [the longest x2 29.5 us: trace_spot(): part_now = lax.ppermute(part_now, axis_name=net_axis, perm=lanes)]
    dynamic_update_slice x0 -> x3, local copies, waits for them, and re-layouts: none -> 3.86 us  [the longest x2 2.53 us: trace_spot(): lax.dynamic_update_slice_in_dim(high, part_now, (local_next - it) % field...]
    dot_general x1, matrix products: 7.75 us -> 4.56 us  [on_device(): jnp.dot(trace_spot(normed), out_weight, preferred_element_type=jnp.float32)]
    ppermute x0 -> x3, starting transfers between devices: none -> 2.68 us  [the longest x1 1.49 us: trace_spot(): kept_arr = lax.ppermute(kept_arr, net_axis, gallery)]
  transfers between devices with their start and end apart: 4 -> 6, of which waited for: 4 -> 5; matrix products, arithmetic and copies ran while one was open for 6% -> 7% of each run, Pallas kernels for 0% -> 0%
where the time goes in v1:
time: 251 us; the launch traced here: 248 us
  waiting for transfers between devices  153 us (61%)
  matrix products  41.2 us (16%)
  blocking collectives  23 us (9%)
  between operations  13.3 us (5%)
  other arithmetic  8.38 us (3%)
  local copies, waits for them, and re-layouts  5.96 us (2%)
  starting transfers between devices  2.76 us (1%)
    all_gather x1, waiting for transfers between devices, side_by_side(): lax.all_gather(both, axis, axis=dim, tiled=True)  96.5 us
    ppermute x2, waiting for transfers between devices, trace_spot(): part_now = lax.ppermute(part_now, axis_name=net_axis, perm=lanes)  29.5 us
    all_gather x2, waiting for transfers between devices, carried_in(): pieces = jax.tree.map(lambda part: lax.all_gather(part, axis), so_far)  27 us
    dot_general x4, matrix products, contract(): return jnp.dot(tokens, piece, preferred_element_type=jnp.float32)  26.1 us
    all_gather x4, blocking collectives, carried_in(): pieces = jax.tree.map(lambda part: lax.all_gather(part, axis), so_far)  23 us
    dot_general x1, matrix products, on_device(): jnp.einsum('hts,shv->thv', attn, value_per_head, preferred_element_type=j...  6.64 us
  transfers between devices with their start and end apart: 6, of which 5 were waited for; matrix products, arithmetic and copies ran while one was open for 7% of the time, Pallas kernels for 0%

profile of v1, /device:TPU:1, one launch (start us, length us, event | category | flops | bytes accessed | tf_op | source)
XLA Modules:
  0.0 247.8 jit_solution(10483470566070652166)
XLA Ops:
  6.5 0.8 copy.26
  7.3 1.6 pad_maximum_fusion
  9.0 0.7 neg.9
  9.7 96.5 %all-gather.8.cloned.1.call-done = bf16[4096,1540]{1,0:T(8,128)(2,1)} async-done(((bf16[64,1540]{1,0:T(8,128)(2,1)}), bf16[4096,1540]{1,0:T(8,128)(2,1)}) %all-gather.8.cloned.1.call-update) | async-done | bytes 12615696 | tf_op jit(solution)/shard_map/all_gather | solution.py:40
  106.2 5.0 %fusion.70 = f32[4,768]{1,0:T(4,128)S(1)} fusion(bf16[768,4096]{1,0:T(8,128)(2,1)} %param.8, bf16[4096,1540]{1,0:T(8,128)(2,1)} %all-gather.8.cloned.1.call-done, f32[4]{0:T(128)S(1)} %neg.9), kind=kOutput, calls=%fused_computation.90 | convolution fusion | flops 25187328 | bytes 7352336 | tf_op jit(solution)/shard_map/dot_general | solution.py:77
  111.2 1.1 reduce-window.6
  113.1 1.8 all-gather.1
  114.9 7.7 %fusion.15 = bf16[512,768]{1,0:T(8,128)(2,1)S(1)} fusion(bf16[768,4096]{1,0:T(8,128)(2,1)} %param.8, bf16[4096,1540]{1,0:T(8,128)(2,1)} %all-gather.8.cloned.1.call-done), kind=kOutput, calls=%fused_computation.21 | convolution fusion | flops 3221618688 | bytes 11272192 | tf_op jit(solution)/shard_map/dot_general | solution.py:77
  122.6 5.9 %fusion.12 = bf16[512,768]{1,0:T(8,128)(2,1)S(1)} fusion(bf16[768,4096]{1,0:T(8,128)(2,1)S(1)} %bitcast.238, bf16[4096,1540]{1,0:T(8,128)(2,1)} %all-gather.8.cloned.1.call-done), kind=kOutput, calls=%fused_computation.20 | convolution fusion | flops 3221618688 | bytes 11272192 | tf_op jit(solution)/shard_map/dot_general | solution.py:77
  128.6 0.4 fusion.23
  128.9 2.2 all-gather
  131.1 0.8 bitcast_add_fusion.8
  132.2 11.3 %all-gather.2 = f32[8,1,4]{2,1,0:T(1,128)S(1)} all-gather(f32[1,1,4]{2,1,0:T(1,128)S(1)} %get-tuple-element.23), channel_id=1, replica_groups=mesh['seq_0'=4,'seq_1'=8,'seq_2'=2,'tp'=4] {'seq_1'}, dimensions={0}, use_global_device_ids=true | all-gather | bytes 144 | tf_op jit(solution)/shard_map/all_gather | solution.py:58
  143.6 21.8 %all-gather.10.cloned.1.call-done = f32[8,4,128,128]{3,2,1,0:T(8,128)} async-done(((f32[1,4,128,128]{3,2,1,0:T(8,128)}), f32[8,4,128,128]{3,2,1,0:T(8,128)}) %all-gather.10.cloned.1.call-update) | async-done | bytes 2097168 | tf_op jit(solution)/shard_map/all_gather | solution.py:58
  165.4 2.4 multiply_add_fusion
  167.8 7.5 %fusion.18 = bf16[512,768]{1,0:T(8,128)(2,1)S(1)} fusion(bf16[768,4096]{1,0:T(8,128)(2,1)} %param.8, bf16[4096,1540]{1,0:T(8,128)(2,1)} %all-gather.8.cloned.1.call-done), kind=kOutput, calls=%fused_computation.22 | convolution fusion | flops 3221618688 | bytes 11272192 | tf_op jit(solution)/shard_map/dot_general | solution.py:77
  175.4 7.7 %all-gather.3 = f32[4,1,4]{2,1,0:T(1,128)S(1)} all-gather(f32[1,1,4]{2,1,0:T(1,128)S(1)} %get-tuple-element.10), channel_id=1, replica_groups=mesh['seq_0'=4,'seq_1'=8,'seq_2'=2,'tp'=4] {'seq_0'}, dimensions={0}, use_global_device_ids=true | all-gather | bytes 80 | tf_op jit(solution)/shard_map/all_gather | solution.py:58
  183.1 0.4 copy.28
  183.5 6.6 %fusion = f32[4,128,768]{2,1,0:T(8,128)} fusion(bf16[768,4,128]{0,2,1:T(8,128)(2,1)} %bitcast.245, f32[4,768]{1,0:T(4,128)S(1)} %get-tuple-element.9, pred[768,768]{1,0:T(8,128)(4,1)S(1)} %iota_compare_fusion, bf16[768,4,128]{0,2,1:T(8,128)(2,1)S(1)} %bitcast.240, bf16[768,4,128]{0,2,1:T(8,128)(2,1)} %bitcast.247), kind=kOutput, calls=%fused_computation.1 | convolution fusion | flops 1219756032 | bytes 4534272 | tf_op jit(solution)/shard_map/hts,shv->thv/dot_general | solution.py:120
  190.1 5.2 %all-gather.12.cloned.1.call-done = f32[4,4,128,128]{3,2,1,0:T(8,128)} async-done(((f32[1,4,128,128]{3,2,1,0:T(8,128)}), f32[4,4,128,128]{3,2,1,0:T(8,128)}) %all-gather.12.cloned.1.call-update) | async-done | bytes 1048592 | tf_op jit(solution)/shard_map/all_gather | solution.py:58
  195.3 3.5 %fusion.11 = (f32[768,4]{0,1:T(4,128)S(1)}, f32[4,128,768]{2,1,0:T(8,128)S(1)}) fusion(f32[4,128,768]{2,1,0:T(8,128)} %fusion, bf16[768,4,128]{2,0,1:T(8,128)(2,1)S(1)} %copy.28, f32[768,4]{0,1:T(4,128)S(1)} %get-tuple-element.8, f32[4,4,128,128]{3,2,1,0:T(8,128)} %all-gather.12.cloned.1.call-done, f32[8,4,128,128]{3,2,1,0:T(8,128)} %all-gather.10.cloned.1.call-done, ...), kind=kOutput, calls=%fused_computation.16 | convolution fusion | flops 105903104 | bytes 7627022 | tf_op jit(solution)/shard_map/fys,ysu->fyu/dot_general | solution.py:106
  199.0 0.2 broadcast_in_dim.18
  199.2 0.3 copy-done
  199.5 1.0 constant_dynamic-update-slice_fusion.3
  200.6 1.2 collective-permute-start
  201.8 1.5 collective-permute-start.1
  203.3 15.2 %collective-permute-done = bf16[768,512]{0,1:T(8,128)(2,1)} collective-permute-done((bf16[768,512]{0,1:T(8,128)(2,1)}, bf16[768,512]{0,1:T(8,128)(2,1)}, u32[]{:S(2)}, u32[]{:S(2)}) %collective-permute-start) | collective-permute-done | bytes 786464 | tf_op jit(solution)/shard_map/ppermute | solution.py:25
  218.5 1.3 constant_dynamic-update-slice_fusion.2
  219.8 1.3 constant_dynamic-update-slice_fusion.1
  221.2 14.3 %collective-permute-done.2 = bf16[768,512]{0,1:T(8,128)(2,1)} collective-permute-done((bf16[768,512]{0,1:T(8,128)(2,1)}, bf16[768,512]{0,1:T(8,128)(2,1)}, u32[]{:S(2)}, u32[]{:S(2)}) %collective-permute-start.2) | collective-permute-done | bytes 786464 | tf_op jit(solution)/shard_map/ppermute | solution.py:25
  235.5 1.2 constant_dynamic-update-slice_fusion
  236.7 4.6 %convolution_convert_fusion = bf16[768,1024]{1,0:T(8,128)(2,1)} fusion(bf16[768,2048]{0,1:T(8,128)(2,1)S(1)} %constant_dynamic-update-slice_fusion, bf16[2048,1024]{1,0:T(8,128)(2,1)S(1)} %copy-done.1), kind=kOutput, calls=%fused_computation.11 | convolution fusion | flops 3222011904 | bytes 8912896 | tf_op jit(solution)/shard_map/dot_general | solution.py:129
  (36 shorter events, 1.2 us)
Async XLA Ops:
  6.5 99.7 %all-gather.8.cloned.1.call-start = ((), (), s32[]{:S(2)}) async-start(), calls=%async_computation | async-start | bytes 13844480 | tf_op jit(solution)/shard_map/all_gather | solution.py:40
  8.9 156.4 %all-gather.10.cloned.1.call-start = ((), (), s32[]{:S(2)}) async-start(), calls=%async_computation.1 | async-start | bytes 2359296 | tf_op jit(solution)/shard_map/all_gather | solution.py:58
  106.2 16.4 %slice-start = ((s8[6291456]{0:T(1024)(128)(4,1)}), s8[2097152]{0:T(1024)(128)(4,1)S(1)}, s32[]{:S(2)}) async-start(s8[6291456]{0:T(1024)(128)(4,1)} %bitcast.237), calls=%async_computation.3 | async-start | bytes 4194304
  114.9 7.7 %slice-start.1 = ((s8[6291456]{0:T(1024)(128)(4,1)}), s8[4194304]{0:T(1024)(128)(4,1)S(1)}, s32[]{:S(2)}) async-start(s8[6291456]{0:T(1024)(128)(4,1)} %bitcast.237), calls=%async_computation.4 | async-start | bytes 8388608
  122.6 6.0 %copy-start.2 = (bf16[512,768]{1,0:T(8,128)(2,1)}, bf16[512,768]{1,0:T(8,128)(2,1)S(1)}, u32[]{:S(2)}) copy-start(bf16[512,768]{1,0:T(8,128)(2,1)S(1)} %fusion.15) | copy-start | bytes 2359300
  128.5 2.6 %copy-start.3 = (bf16[512,768]{1,0:T(8,128)(2,1)}, bf16[512,768]{1,0:T(8,128)(2,1)S(1)}, u32[]{:S(2)}) copy-start(bf16[512,768]{1,0:T(8,128)(2,1)S(1)} %fusion.12) | copy-start | bytes 2359300
  131.9 63.4 %all-gather.12.cloned.1.call-start = ((), (), s32[]{:S(2)}) async-start(), calls=%async_computation.2 | async-start | bytes 1310720 | tf_op jit(solution)/shard_map/all_gather | solution.py:58
  198.9 0.7 copy-start
  200.6 17.9 %collective-permute-start = (bf16[768,512]{0,1:T(8,128)(2,1)}, bf16[768,512]{0,1:T(8,128)(2,1)}, u32[]{:S(2)}, u32[]{:S(2)}) collective-permute-start(bf16[768,512]{0,1:T(8,128)(2,1)} %get-tuple-element.29), channel_id=1, source_target_pairs={{0,1},{1,2},{2,3},{3,0},{4,5},{5,6},{6,7},{7,4},{8,9},{9,10},{10,1... | collective-permute-start | bytes 2359304 | tf_op jit(solution)/shard_map/ppermute | solution.py:25
  201.8 18.0 %collective-permute-start.1 = (bf16[768,512]{0,1:T(8,128)(2,1)}, bf16[768,512]{0,1:T(8,128)(2,1)}, u32[]{:S(2)}, u32[]{:S(2)}) collective-permute-start(bf16[768,512]{0,1:T(8,128)(2,1)} %get-tuple-element.29), channel_id=1, source_target_pairs={{0,3},{1,0},{2,1},{3,2},{4,7},{5,4},{6,5},{7,6},{8,11},{9,8},{10,9... | collective-permute-start | bytes 2359304 | tf_op jit(solution)/shard_map/ppermute | solution.py:30
  218.5 17.0 %collective-permute-start.2 = (bf16[768,512]{0,1:T(8,128)(2,1)}, bf16[768,512]{0,1:T(8,128)(2,1)}, u32[]{:S(2)}, u32[]{:S(2)}) collective-permute-start(bf16[768,512]{0,1:T(8,128)(2,1)} %collective-permute-done), channel_id=1, source_target_pairs={{0,1},{1,2},{2,3},{3,0},{4,5},{5,6},{6,7},{7,4},{8,9},{9,10},{10,1... | collective-permute-start | bytes 2359304 | tf_op jit(solution)/shard_map/ppermute | solution.py:25
  218.5 18.2 %copy-start.1 = (bf16[2048,1024]{1,0:T(8,128)(2,1)S(1)}, bf16[2048,1024]{1,0:T(8,128)(2,1)}, u32[]{:S(2)}) copy-start(bf16[2048,1024]{1,0:T(8,128)(2,1)} %param.15) | copy-start | bytes 12582916
Sparse Core Ops, SparseCore 0:
  10.1 96.0 all-gather.7
  132.1 33.2 all-gather.9
  167.9 27.3 all-gather.11
